TPU v7x, 32 devices: a whole 2x2x4 slice. The times are simulated.
32 devices in a mesh: dp: 8 (over y, x, core), expert: 4 (over z).
Axes of the slice: x: 2, y: 2, z: 4, core: 2. Of those that a mesh axis runs over, the one named last changes fastest.
Arguments:
- out_grad: bfloat16 [64, 4096], P(('dp', 'expert')), may hold values from -0.29882812 to 0.29882812
- routes: int32 [64, 2], P('dp'), may hold values from 0 to 7, all different within a row; in each aligned block of 8 rows (0 to 7, 8 to 15, ...) at most 3 rows name the same one
- gate_values: bfloat16 [64, 2], P(('dp', 'expert')), may hold values from 0.099609375 to 1
- gate_pre: bfloat16 [8, 24, 12288], P('expert', None, 'dp'), may hold values from -6 to 6
- up_pre: bfloat16 [8, 24, 12288], P('expert', None, 'dp'), may hold values from -6 to 6
- w_down: bfloat16 [8, 12288, 4096], P('expert', 'dp'), may hold values from -0.0546875 to 0.0546875
Outputs:
- grad_gates: float32 [64, 2], P(('dp', 'expert'))
- grad_gate_pre: bfloat16 [8, 24, 12288], P('expert', None, 'dp')
- grad_up_pre: bfloat16 [8, 24, 12288], P('expert', None, 'dp')
- grad_down: bfloat16 [8, 12288, 4096], P('expert', 'dp')
Inputs may be any that keep to these rules, and one draw needn't show every extreme that they name: `routes`: each token names two different experts. Among the 8 tokens of one block (aligned blocks of tokens, one for each dp index) no expert is named more than 3 times, and some expert reaches 3 in some block.
All inputs are finite; a program needn't handle non-finite values.
Results may differ from a plain program's by a relative error of at most 0.0049.
Values may be sent and summed in bfloat16 or wider, within the bound.
A program may use at most 128 MiB of HBM per device.

v0:
```python
import jax
import jax.numpy as jnp
from jax import lax
from jax.sharding import PartitionSpec as P

SLOTS = 3


def expert_terms(gate_piece, up_piece, weights, rows_in, gate_row):
    projected = jnp.einsum("erd,efd->erf", rows_in, weights, preferred_element_type=jnp.float32)
    gate_act = gate_piece.astype(jnp.float32)
    up_act = up_piece.astype(jnp.float32)
    sigmoid_val = jax.nn.sigmoid(gate_act)
    silu_val = gate_act * sigmoid_val
    hidden = silu_val * up_act
    partial_value = jnp.sum(hidden * projected, axis=2)
    scale_col = gate_row.astype(jnp.float32)[:, :, None]
    weighted = (scale_col * hidden).astype(jnp.bfloat16)
    down_term = jnp.einsum("erf,erd->efd", weighted, rows_in, preferred_element_type=jnp.float32)
    grad_hidden = scale_col * projected
    grad_gate = (
        grad_hidden * up_act * sigmoid_val * (1.0 + gate_act * (1.0 - sigmoid_val))
    ).astype(jnp.bfloat16)
    grad_up = (grad_hidden * silu_val).astype(jnp.bfloat16)
    return (partial_value, grad_gate, grad_up, down_term)


def per_device(out_grad, routes, gate_values, gate_pre, up_pre, w_down):
    groups = lax.axis_size("expert")
    local_count = gate_pre.shape[0]
    experts = local_count * groups
    tok_count = out_grad.shape[0]
    my_rank = lax.axis_index("expert")
    flat_routes = routes.reshape(-1)
    onehot = (flat_routes[:, None] == jnp.arange(experts, dtype=jnp.int32)[None, :]).astype(
        jnp.int32
    )
    position = jnp.sum((jnp.cumsum(onehot, axis=0) - 1) * onehot, axis=1)
    own_expert = lax.dynamic_slice_in_dim(flat_routes, my_rank * tok_count * 2, tok_count * 2)
    own_position = lax.dynamic_slice_in_dim(position, my_rank * tok_count * 2, tok_count * 2)
    target = own_expert * SLOTS + own_position
    selector = target[:, None] == jnp.arange(experts * SLOTS, dtype=jnp.int32)[None, :]
    picker = selector.astype(jnp.bfloat16).T
    pair_rows = jnp.repeat(out_grad, 2, axis=0)
    send_rows = (
        jnp.dot(picker, pair_rows, preferred_element_type=jnp.float32)
        .astype(jnp.bfloat16)
        .reshape(experts, SLOTS, -1)
    )
    send_gates = (
        jnp.dot(picker, gate_values.reshape(-1, 1), preferred_element_type=jnp.float32)
        .astype(jnp.bfloat16)
        .reshape(experts, SLOTS)
    )
    got_rows, got_gates = (
        lax.all_to_all(send_rows, "expert", split_axis=0, concat_axis=0, tiled=True),
        lax.all_to_all(send_gates, "expert", split_axis=0, concat_axis=0, tiled=True),
    )
    dispatched = jnp.sum(
        got_rows.reshape(groups, local_count, SLOTS, -1).astype(jnp.float32), axis=0
    ).astype(jnp.bfloat16)
    slot_gate = jnp.sum(
        got_gates.reshape(groups, local_count, SLOTS).astype(jnp.float32), axis=0
    ).astype(jnp.bfloat16)
    all_rows, all_gates = (
        lax.all_gather(dispatched, "dp", axis=1, tiled=True),
        lax.all_gather(slot_gate, "dp", axis=1, tiled=True),
    )
    partial_value, grad_gate_pre, grad_up_pre, down_sum = expert_terms(
        gate_pre, up_pre, w_down, all_rows, all_gates
    )
    grad_down = down_sum.astype(jnp.bfloat16)
    own_sums = lax.psum_scatter(partial_value, "dp", scatter_dimension=1, tiled=True)
    score_table = lax.all_gather(own_sums, "expert", axis=0, tiled=True)
    picked = jnp.sum(jnp.where(selector, score_table.reshape(1, -1), 0.0), axis=1)
    grad_gates = picked.reshape(tok_count, 2)
    return (grad_gates, grad_gate_pre, grad_up_pre, grad_down)


def solution(mesh):
    return jax.shard_map(
        per_device,
        mesh=mesh,
        in_specs=(
            P(("dp", "expert"), None),
            P("dp", None),
            P(("dp", "expert"), None),
            P("expert", None, "dp"),
            P("expert", None, "dp"),
            P("expert", "dp", None),
        ),
        out_specs=(
            P(("dp", "expert"), None),
            P("expert", None, "dp"),
            P("expert", None, "dp"),
            P("expert", "dp", None),
        ),
        check_vma=False,
    )
```

profile of v0, /device:TPU:0, one launch (start us, length us, event | category | flops | bytes accessed | tf_op | source)
XLA Modules:
  0.0 90.1 jit_solution(11109516635984574383)
XLA Ops:
  0.6 0.7 reshape.54
  1.4 0.8 copy.28
  2.3 0.2 select_reduce_fusion
  2.6 0.2 fusion
  2.8 0.7 all_to_all.10
  3.5 6.3 %all-to-all-start.1 = ((bf16[4,2,3]{2,1,0:T(2,128)(2,1)}), bf16[4,2,3]{2,1,0:T(2,128)(2,1)S(1)}, u32[]{:S(2)}, u32[]{:S(2)}) async-start(bf16[4,2,3]{2,1,0:T(2,128)(2,1)} %all_to_all.10), calls=%async_computation.1 | async-start | bytes 4096 | tf_op jit(solution)/shard_map/all_to_all | solution.py:57
  9.8 0.7 broadcast_in_dim.21
  10.6 0.3 convolution_convert_fusion.1
  10.9 0.8 reshape.44
  11.8 3.5 %all-to-all-done.1 = bf16[4,2,3]{2,1,0:T(2,128)(2,1)S(1)} async-done(((bf16[4,2,3]{2,1,0:T(2,128)(2,1)}), bf16[4,2,3]{2,1,0:T(2,128)(2,1)S(1)}, u32[]{:S(2)}, u32[]{:S(2)}) %all-to-all-start.1) | async-done | bytes 80 | tf_op jit(solution)/shard_map/all_to_all | solution.py:57
  15.3 3.4 %all-to-all-start = ((bf16[8,3,4096]{2,1,0:T(4,128)(2,1)}), bf16[8,3,4096]{2,1,0:T(4,128)(2,1)S(1)}, u32[]{:S(2)}, u32[]{:S(2)}) async-start(bf16[8,3,4096]{2,1,0:T(4,128)(2,1)} %reshape.44), calls=%async_computation | async-start | bytes 524288 | tf_op jit(solution)/shard_map/all_to_all | solution.py:56
  18.7 1.2 %dynamic-slice = u32[1]{0:T(128)} dynamic-slice(u32[32]{0:T(128)} %constant.34, u32[]{:T(128)S(6)} %add.21), dynamic_slice_sizes={1} | dynamic-slice | bytes 12
  20.6 8.8 %all-gather.1 = bf16[8,3,2]{1,2,0:T(2,128)(2,1)S(1)} all-gather(bf16[1,3,2]{1,2,0:T(2,128)(2,1)S(1)} %bitcast.22), channel_id=1, replica_groups=mesh['dp'=8,'expert'=4] {'dp'}, dimensions={0}, use_global_device_ids=true | all-gather | bytes 108 | tf_op jit(solution)/shard_map/all_gather | solution.py:67
  29.4 0.1 copy.31
  29.5 0.1 copy.32
  29.7 0.1 reduce_sum.52
  29.9 9.6 %all_gather.9 = bf16[2,24,4096]{2,0,1:T(2,128)(2,1)S(1)} all-gather(bf16[2,3,4096]{2,0,1:T(2,128)(2,1)S(1)} %copy.29), channel_id=1, replica_groups=mesh['dp'=8,'expert'=4] {'dp'}, dimensions={1}, use_global_device_ids=true | all-gather | bytes 442368 | tf_op jit(solution)/shard_map/all_gather | solution.py:66
  39.5 12.6 %fusion.6 = (bf16[2,24,1536]{2,1,0:T(8,128)(2,1)}, f32[2,24]{1,0:T(2,128)S(1)}, bf16[2,24,1536]{2,1,0:T(8,128)(2,1)}) fusion(bf16[2,24,1536]{2,1,0:T(8,128)(2,1)} %param.10, bf16[2,24,1536]{2,1,0:T(8,128)(2,1)} %param.9, f32[2,24]{1,0:T(2,128)S(1)} %bitcast.20, bf16[2,1536,4096]{2,1,0:T(8,128)(2,1)} %param.11, bf16[2,24,4096]{2,0,1:T(2,128)(2,1)S(1)} %all_gather.9), kind=kOutput, calls=%fused_computation.14 | convolution fusion | flops 605380544 | bytes 26149248 | tf_op jit(solution)/shard_map/erd,efd->erf/dot_general | solution.py:10
  52.0 13.2 %all-reduce = f32[2,24]{1,0:T(2,128)S(1)} all-reduce(f32[2,24]{1,0:T(2,128)S(1)} %get-tuple-element.5), channel_id=2, replica_groups=mesh['dp'=8,'expert'=4] {'dp'}, use_global_device_ids=true, to_apply=%region_4.5.clone | all-reduce | flops 48 | bytes 384
  65.3 12.5 %convolution_convert_fusion = bf16[2,1536,4096]{2,1,0:T(8,128)(2,1)} fusion(bf16[2,24,4096]{2,0,1:T(2,128)(2,1)S(1)} %all_gather.9, bf16[2,24,1536]{2,1,0:T(8,128)(2,1)S(1)} %copy-done, f32[2,24]{1,0:T(2,128)S(1)} %bitcast.21, bf16[2,24,1536]{2,1,0:T(8,128)(2,1)S(1)} %copy-done.1), kind=kOutput, calls=%fused_computation | convolution fusion | flops 617226240 | bytes 25854144 | tf_op jit(solution)/shard_map/erf,erd->efd/dot_general | solution.py:19
  77.8 11.3 %all-gather = f32[4,2,3]{2,1,0:T(2,128)S(1)} all-gather(f32[1,2,3]{2,1,0:T(2,128)S(1)} %dynamic-slice_bitcast_fusion), channel_id=1, replica_groups=mesh['dp'=8,'expert'=4] {'expert'}, dimensions={0}, use_global_device_ids=true | all-gather | bytes 120 | tf_op jit(solution)/shard_map/all_gather | solution.py:74
  89.1 0.1 broadcast_in_dim.22
  89.2 0.2 select_reduce_fusion.1
  89.4 0.7 reshape.46
  (14 shorter events, 0.5 us)
Async XLA Ops:
  3.5 11.8 %all-to-all-start.1 = ((bf16[4,2,3]{2,1,0:T(2,128)(2,1)}), bf16[4,2,3]{2,1,0:T(2,128)(2,1)S(1)}, u32[]{:S(2)}, u32[]{:S(2)}) async-start(bf16[4,2,3]{2,1,0:T(2,128)(2,1)} %all_to_all.10), calls=%async_computation.1 | async-start | bytes 4096 | tf_op jit(solution)/shard_map/all_to_all | solution.py:57
  10.6 54.8 %copy-start = (bf16[2,24,1536]{2,1,0:T(8,128)(2,1)S(1)}, bf16[2,24,1536]{2,1,0:T(8,128)(2,1)}, u32[]{:S(2)}) copy-start(bf16[2,24,1536]{2,1,0:T(8,128)(2,1)} %param.10) | copy-start | bytes 442372
  10.6 54.8 %copy-start.1 = (bf16[2,24,1536]{2,1,0:T(8,128)(2,1)S(1)}, bf16[2,24,1536]{2,1,0:T(8,128)(2,1)}, u32[]{:S(2)}) copy-start(bf16[2,24,1536]{2,1,0:T(8,128)(2,1)} %param.9) | copy-start | bytes 442372
  15.3 14.4 %all-to-all-start = ((bf16[8,3,4096]{2,1,0:T(4,128)(2,1)}), bf16[8,3,4096]{2,1,0:T(4,128)(2,1)S(1)}, u32[]{:S(2)}, u32[]{:S(2)}) async-start(bf16[8,3,4096]{2,1,0:T(4,128)(2,1)} %reshape.44), calls=%async_computation | async-start | bytes 524288 | tf_op jit(solution)/shard_map/all_to_all | solution.py:56
where the time goes:
time: 90.5 us; the launch traced here: 90.1 us
  blocking collectives  42.9 us (47%)
  matrix products  25.6 us (28%)
  starting transfers between devices  9.75 us (11%)
  local copies, waits for them, and re-layouts  6.25 us (7%)
  waiting for transfers between devices  3.54 us (4%)
  between operations  1.36 us (2%)
    unnamed x1, blocking collectives  13.2 us
    dot_general x1, matrix products, expert_terms(): jnp.einsum('erd,efd->erf', rows_in, weights, preferred_element_type=jnp.f...  12.6 us
    dot_general x1, matrix products, expert_terms(): jnp.einsum('erf,erd->efd', weighted, rows_in, preferred_element_type=jnp....  12.5 us
    all_gather x1, blocking collectives, per_device(): score_table = lax.all_gather(own_sums, 'expert', axis=0, tiled=True)  11.3 us
    all_gather x1, blocking collectives, per_device(): lax.all_gather(dispatched, 'dp', axis=1, tiled=True)  9.56 us
    all_gather x1, blocking collectives, per_device(): lax.all_gather(slot_gate, 'dp', axis=1, tiled=True)  8.8 us
    all_to_all x1, starting transfers between devices, per_device(): lax.all_to_all(send_gates, 'expert', split_axis=0, concat_axis=0, tiled=T...  6.35 us
    all_to_all x1, waiting for transfers between devices, per_device(): lax.all_to_all(send_gates, 'expert', split_axis=0, concat_axis=0, tiled=T...  3.54 us
  transfers between devices with their start and end apart: 2, of which 1 were waited for; matrix products, arithmetic and copies ran while one was open for 4% of the time, Pallas kernels for 0%

commit v1 on v0

--- a/solution.py
+++ b/solution.py
@@ -1,6 +1,10 @@
+import functools
+
 import jax
 import jax.numpy as jnp
 from jax import lax
+from jax.experimental import pallas as pl
+from jax.experimental.pallas import tpu as pltpu
 from jax.sharding import PartitionSpec as P
 
 SLOTS = 3
@@ -25,7 +29,7 @@
     return (partial_value, grad_gate, grad_up, down_term)
 
 
-def per_device(out_grad, routes, gate_values, gate_pre, up_pre, w_down):
+def general_device(out_grad, routes, gate_values, gate_pre, up_pre, w_down):
     groups = lax.axis_size("expert")
     local_count = gate_pre.shape[0]
     experts = local_count * groups
@@ -77,6 +81,335 @@
     return (grad_gates, grad_gate_pre, grad_up_pre, grad_down)
 
 
+LANES = 128
+CORES = 2
+MESH = pl.DeviceIdType.MESH
+
+
+def pow2(n):
+    return n & (n - 1) == 0
+
+
+def fused_fits(n_dp, groups, tokens, width, local, rows, hidden):
+    if 16 % tokens or n_dp % CORES:
+        return False
+    split = 16 // tokens
+    padded = -(-rows // 16) * 16
+    return (
+        width % (split * LANES) == 0
+        and hidden % 512 == 0
+        and local * padded <= LANES
+        and pow2(split)
+        and pow2(groups)
+        and n_dp * groups <= 64
+        and rows == n_dp * SLOTS
+        and local * hidden * width * 2 <= 32 << 20
+    )
+
+
+def gather_project(
+    n_dp, groups, split, local, rows, padded, block,
+    payload, gate_pre, up_pre, weights,
+    rows_out, gates_out, proj_out, grads_out,
+    table, held, sums_own, sums_all,
+    load_sem, own_sem, send_z, recv_z, send_c, recv_c, send_p, recv_p, send_s, recv_s,
+):
+    me_dp, me_z = lax.axis_index("dp"), lax.axis_index("expert")
+    total = n_dp * groups
+    me = me_dp * groups + me_z
+    chips = n_dp // CORES
+    chip, core = me_dp // CORES, lax.rem(me_dp, CORES)
+    hidden = held.shape[1]
+    per = hidden // block
+    chunk = payload.shape[1] - LANES
+
+    loads = []
+    for e in range(local):
+        for b in range(per):
+            copy = pltpu.make_async_copy(
+                weights.at[e, pl.ds(b * block, block)],
+                held.at[e, pl.ds(b * block, block)],
+                load_sem.at[e * per + b],
+            )
+            copy.start()
+            loads.append(copy)
+    keep = pltpu.make_async_copy(payload, table.at[me], own_sem)
+    keep.start()
+
+    barrier = pltpu.get_barrier_semaphore()
+    for off in range(1, total):
+        other = lax.rem(me + off, total)
+        pl.semaphore_signal(
+            barrier, inc=1, device_id=(other // groups, lax.rem(other, groups)), device_id_type=MESH
+        )
+    pl.semaphore_wait(barrier, total - 1)
+
+    sent = []
+    first = []
+    for dz in range(1, groups):
+        copy = pltpu.make_async_remote_copy(
+            src_ref=payload,
+            dst_ref=table.at[me],
+            send_sem=send_z.at[dz],
+            recv_sem=recv_z.at[dz],
+            device_id=(me_dp, lax.rem(me_z + dz, groups)),
+            device_id_type=MESH,
+        )
+        copy.start()
+        first.append(copy)
+    sent += first
+    keep.wait()
+    for copy in first:
+        copy.wait_recv()
+
+    def block_copy(dp_index, target, s_sem, r_sem):
+        copy = pltpu.make_async_remote_copy(
+            src_ref=table.at[pl.ds(dp_index * groups, groups)],
+            dst_ref=table.at[pl.ds(dp_index * groups, groups)],
+            send_sem=s_sem,
+            recv_sem=r_sem,
+            device_id=(target, me_z),
+            device_id_type=MESH,
+        )
+        copy.start()
+        return copy
+
+    second = []
+    for dc in range(1, chips):
+        target = lax.rem(chip + dc, chips) * CORES + core
+        second.append(block_copy(me_dp, target, send_c.at[dc], recv_c.at[dc]))
+    partner = chip * CORES + (1 - core)
+    third = [block_copy(me_dp, partner, send_p.at[0], recv_p.at[0])]
+    for dc in range(1, chips):
+        second[dc - 1].wait_recv()
+        source = lax.rem(chip - dc + chips, chips) * CORES + core
+        third.append(block_copy(source, partner, send_p.at[dc], recv_p.at[dc]))
+    for copy in third:
+        copy.wait_recv()
+    sent += second + third
+
+    depth = total * 16
+    wide = local * padded
+    data = table[...].reshape(depth, chunk + LANES)
+    meta_low = data[:, chunk:]
+    meta = meta_low.astype(jnp.float32)
+    row = lax.broadcasted_iota(jnp.int32, (depth, 1), 0)
+    piece = (row & (split - 1)).astype(jnp.float32)
+    col = lax.broadcasted_iota(jnp.int32, (depth, split * wide), 1).astype(jnp.float32)
+    low = (me_z * local).astype(jnp.float32)
+    picks = []
+    for k in range(2):
+        offset = meta[:, 2 * k : 2 * k + 1] - low
+        code = piece * wide + offset * padded + meta[:, 2 * k + 1 : 2 * k + 2]
+        code = jnp.where((offset >= 0) & (offset < local), code, -1.0)
+        picks.append(jnp.where(col == code, 1.0, 0.0))
+    either = (picks[0] + picks[1]).T.astype(jnp.bfloat16)
+    slots = jnp.dot(either, data[:, :chunk], preferred_element_type=jnp.float32).astype(jnp.bfloat16)
+    for c in range(split):
+        for e in range(local):
+            at = c * wide + e * padded
+            rows_out[e, :, c * chunk : (c + 1) * chunk] = slots[at : at + padded]
+    scale = jnp.zeros((wide, 1), jnp.float32)
+    for k in range(2):
+        pick = picks[k][:, :LANES].T.astype(jnp.bfloat16)
+        got = jnp.dot(pick, meta_low, preferred_element_type=jnp.float32)
+        scale = scale + got[:wide, 4 + k : 5 + k]
+    for e in range(local):
+        gates_out[e] = jnp.broadcast_to(scale[e * padded : (e + 1) * padded], (padded, LANES))
+
+    lane = lax.broadcasted_iota(jnp.int32, (rows, LANES), 1)
+    slot = lax.broadcasted_iota(jnp.int32, (rows, LANES), 0)
+    mine = jnp.zeros((1, LANES), jnp.float32)
+    for e in range(local):
+        part = jnp.zeros((rows, 1), jnp.float32)
+        for b in range(per):
+            loads[e * per + b].wait()
+            span = slice(b * block, (b + 1) * block)
+            proj = lax.dot_general(
+                rows_out[e], held[e, span], (((1,), (1,)), ((), ())),
+                preferred_element_type=jnp.float32,
+            )[:rows]
+            proj_out[e, :, span] = proj
+            gate_act = gate_pre[e, :, span].astype(jnp.float32)
+            up_act = up_pre[e, :, span].astype(jnp.float32)
+            silu_val = gate_act * jax.nn.sigmoid(gate_act)
+            part = part + jnp.sum(silu_val * up_act * proj, axis=1, keepdims=True)
+        mine = mine + jnp.sum(
+            jnp.where(lane == slot + e * padded, part, 0.0), axis=0, keepdims=True
+        )
+    sums_own[...] = mine
+    sums_all[me] = mine
+    last = []
+    for off in range(1, total):
+        other = lax.rem(me + off, total)
+        copy = pltpu.make_async_remote_copy(
+            src_ref=sums_own,
+            dst_ref=sums_all.at[me],
+            send_sem=send_s.at[off],
+            recv_sem=recv_s.at[off],
+            device_id=(other // groups, lax.rem(other, groups)),
+            device_id_type=MESH,
+        )
+        copy.start()
+        last.append(copy)
+    for copy in last:
+        copy.wait_recv()
+    sent += last
+
+    own = payload[:, chunk:].astype(jnp.float32)
+    lane_at = lax.broadcasted_iota(jnp.int32, (1, LANES), 1)
+    out_row = lax.broadcasted_iota(jnp.int32, grads_out.shape, 0)
+    out_col = lax.broadcasted_iota(jnp.int32, grads_out.shape, 1)
+    by_group = []
+    for z in range(groups):
+        acc = sums_all[z]
+        for d in range(1, n_dp):
+            acc = acc + sums_all[d * groups + z]
+        by_group.append(acc)
+    result = jnp.zeros(grads_out.shape, jnp.float32)
+    for t in range(16 // split):
+        for k in range(2):
+            expert = own[t * split : t * split + 1, 2 * k : 2 * k + 1]
+            spot = own[t * split : t * split + 1, 2 * k + 1 : 2 * k + 2]
+            value = jnp.zeros((1, LANES), jnp.float32)
+            for z in range(groups):
+                offset = expert - z * local
+                code = jnp.where((offset >= 0) & (offset < local), offset * padded + spot, -1.0)
+                value = value + jnp.where(lane_at.astype(jnp.float32) == code, by_group[z], 0.0)
+            value = jnp.sum(value, axis=1, keepdims=True)
+            result = jnp.where((out_row == t) & (out_col == k), value, result)
+    grads_out[...] = result
+    for copy in sent:
+        copy.wait_send()
+
+
+def finish(
+    rows, proj, rows_in, gates, gate_pre, up_pre, sums, grad_gate, grad_up, grad_down, grad_sums
+):
+    grad_sums[...] = sums[...]
+    gate_act = gate_pre[0].astype(jnp.float32)
+    up_act = up_pre[0].astype(jnp.float32)
+    sigmoid_val = jax.nn.sigmoid(gate_act)
+    silu_val = gate_act * sigmoid_val
+    scale = gates[0, :rows, 0:1]
+    grad_hidden = scale * proj[0]
+    grad_gate[0] = (
+        grad_hidden * up_act * sigmoid_val * (1.0 + gate_act * (1.0 - sigmoid_val))
+    ).astype(jnp.bfloat16)
+    grad_up[0] = (grad_hidden * silu_val).astype(jnp.bfloat16)
+    weighted = scale * (silu_val * up_act)
+    fill = rows_in.shape[1] - rows
+    if fill:
+        weighted = jnp.concatenate(
+            [weighted, jnp.zeros((fill, weighted.shape[1]), jnp.float32)], axis=0
+        )
+    turned = weighted.T.astype(jnp.bfloat16)
+    step = 512
+    for c in range(0, rows_in.shape[2], step):
+        grad_down[0, :, c : c + step] = jnp.dot(
+            turned, rows_in[0, :, c : c + step], preferred_element_type=jnp.float32
+        ).astype(jnp.bfloat16)
+
+
+def fused_device(out_grad, routes, gate_values, gate_pre, up_pre, w_down):
+    n_dp, groups = lax.axis_size("dp"), lax.axis_size("expert")
+    tokens, width = out_grad.shape
+    local, rows, hidden = gate_pre.shape
+    split = 16 // tokens
+    chunk = width // split
+    padded = -(-rows // 16) * 16
+    block = 512
+    total = n_dp * groups
+    me_dp, me_z = lax.axis_index("dp"), lax.axis_index("expert")
+
+    flat = routes.reshape(-1)
+    count = flat.shape[0]
+    earlier = jnp.arange(count)[None, :] < jnp.arange(count)[:, None]
+    position = jnp.sum(((flat[:, None] == flat[None, :]) & earlier).astype(jnp.int32), axis=1)
+    both = jnp.stack([flat, position + me_dp * SLOTS], axis=1).reshape(groups, tokens, 4)
+    pick = (jnp.arange(groups) == me_z)[:, None, None]
+    codes = jnp.sum(jnp.where(pick, both, 0), axis=0).astype(jnp.bfloat16)
+    meta = jnp.concatenate([codes, gate_values], axis=1)
+    meta = jnp.pad(meta, ((0, 0), (0, LANES - 6)))
+    meta = jnp.broadcast_to(meta[:, None, :], (tokens, split, LANES)).reshape(16, LANES)
+    payload = jnp.concatenate([out_grad.reshape(16, chunk), meta], axis=1)
+
+    vmem = pl.BlockSpec(memory_space=pltpu.VMEM)
+    dma = pltpu.SemaphoreType.DMA
+    chips = n_dp // CORES
+    rows_in, gates, proj, sums = pl.pallas_call(
+        functools.partial(
+            gather_project, n_dp, groups, split, local, rows, padded, block
+        ),
+        out_shape=(
+            jax.ShapeDtypeStruct((local, padded, width), jnp.bfloat16),
+            jax.ShapeDtypeStruct((local, padded, LANES), jnp.float32),
+            jax.ShapeDtypeStruct((local, rows, hidden), jnp.float32),
+            jax.ShapeDtypeStruct((tokens, 2), jnp.float32),
+        ),
+        in_specs=[vmem, vmem, vmem, pl.BlockSpec(memory_space=pl.ANY)],
+        out_specs=(vmem, vmem, vmem, vmem),
+        scratch_shapes=[
+            pltpu.VMEM((total, 16, chunk + LANES), jnp.bfloat16),
+            pltpu.VMEM((local, hidden, width), jnp.bfloat16),
+            pltpu.VMEM((1, LANES), jnp.float32),
+            pltpu.VMEM((total, 1, LANES), jnp.float32),
+            dma((local * hidden // block,)),
+            dma,
+            dma((groups,)),
+            dma((groups,)),
+            dma((chips,)),
+            dma((chips,)),
+            dma((chips,)),
+            dma((chips,)),
+            dma((total,)),
+            dma((total,)),
+        ],
+        compiler_params=pltpu.CompilerParams(
+            collective_id=0, has_side_effects=True, vmem_limit_bytes=60 << 20
+        ),
+        name="gather_project",
+    )(payload, gate_pre, up_pre, w_down)
+
+    piece = 256
+    small = pl.BlockSpec((1, rows, piece), lambda e, b: (e, 0, b))
+    grad_gate_pre, grad_up_pre, grad_down, grad_gates = pl.pallas_call(
+        functools.partial(finish, rows),
+        grid=(local, hidden // piece),
+        out_shape=(
+            jax.ShapeDtypeStruct(gate_pre.shape, jnp.bfloat16),
+            jax.ShapeDtypeStruct(gate_pre.shape, jnp.bfloat16),
+            jax.ShapeDtypeStruct(w_down.shape, jnp.bfloat16),
+            jax.ShapeDtypeStruct((tokens, 2), jnp.float32),
+        ),
+        in_specs=[
+            small,
+            pl.BlockSpec((1, padded, width), lambda e, b: (e, 0, 0)),
+            pl.BlockSpec((1, padded, LANES), lambda e, b: (e, 0, 0)),
+            small,
+            small,
+            pl.BlockSpec((tokens, 2), lambda e, b: (0, 0)),
+        ],
+        out_specs=(
+            small,
+            small,
+            pl.BlockSpec((1, piece, width), lambda e, b: (e, b, 0)),
+            pl.BlockSpec((tokens, 2), lambda e, b: (0, 0)),
+        ),
+        compiler_params=pltpu.CompilerParams(vmem_limit_bytes=60 << 20),
+        name="finish",
+    )(proj, rows_in, gates, gate_pre, up_pre, sums)
+    return grad_gates, grad_gate_pre, grad_up_pre, grad_down
+
+
+def per_device(out_grad, routes, gate_values, gate_pre, up_pre, w_down):
+    fits = fused_fits(
+        lax.axis_size("dp"), lax.axis_size("expert"), *out_grad.shape, *gate_pre.shape
+    )
+    chosen = fused_device if fits else general_device
+    return chosen(out_grad, routes, gate_values, gate_pre, up_pre, w_down)
+
+
 def solution(mesh):
     return jax.shard_map(
         per_device,

time: 90.5 us -> 53.3 us (0.59)
  Pallas kernels: 0 us -> 48.6 us
  blocking collectives: 42.9 us -> 0 us
  matrix products: 25.6 us -> 0 us
  starting transfers between devices: 9.75 us -> 0 us
  local copies, waits for them, and re-layouts: 6.25 us -> 1.82 us
  waiting for transfers between devices: 3.54 us -> 0 us
  other arithmetic: 0.71 us -> 1.64 us
    pallas_call x0 -> x2, Pallas kernels: none -> 48.6 us  [the longest x1 33.9 us: fused_device(): pl.pallas_call(functools.partial(gather_project, n_dp, groups, split, loc...]
    all_gather x3 -> x0, blocking collectives: 29.7 us -> none  [the longest x1 11.3 us: per_device(): score_table = lax.all_gather(own_sums, 'expert', axis=0, tiled=True)]
    dot_general x4 -> x0, matrix products: 25.6 us -> none  [the longest x1 12.6 us: expert_terms(): jnp.einsum('erd,efd->erf', rows_in, weights, preferred_element_type=jnp.f...]
    unnamed x1 -> x0, blocking collectives: 13.2 us -> none
    all_to_all x2 -> x0, starting transfers between devices: 9.75 us -> none  [the longest x1 6.35 us: per_device(): lax.all_to_all(send_gates, 'expert', split_axis=0, concat_axis=0, tiled=T...]
    all_to_all x2 -> x0, waiting for transfers between devices: 3.54 us -> none  [the longest x1 3.54 us: per_device(): lax.all_to_all(send_gates, 'expert', split_axis=0, concat_axis=0, tiled=T...]
    reshape x5 -> x3, local copies, waits for them, and re-layouts: 2.33 us -> 0.82 us  [the longest x1 0.73 us: fused_device(): payload = jnp.concatenate([out_grad.reshape(16, chunk), meta], axis=1)]
    concatenate x0 -> x2, other arithmetic: none -> 1.35 us  [the longest x1 0.74 us: fused_device(): meta = jnp.concatenate([codes, gate_values], axis=1)]
  transfers between devices with their start and end apart: 2 -> 0, of which waited for: 1 -> 0; matrix products, arithmetic and copies ran while one was open for 4% -> 0% of each run, Pallas kernels for 0% -> 0%
where the time goes in v1:
time: 53.3 us; the launch traced here: 52.7 us
  Pallas kernels  48.6 us (91%)
  local copies, waits for them, and re-layouts  1.82 us (3%)
  other arithmetic  1.64 us (3%)
  between operations  0.67 us (1%)
    pallas_call x1, Pallas kernels, fused_device(): pl.pallas_call(functools.partial(gather_project, n_dp, groups, split, loc...  33.9 us
    pallas_call x1, Pallas kernels, fused_device(): pl.pallas_call(functools.partial(finish, rows), grid=(local, hidden // pi...  14.7 us

profile of v1, /device:TPU:0, one launch (start us, length us, event | category | flops | bytes accessed | tf_op | source)
XLA Modules:
  0.0 52.7 jit_solution(15110657376283234297)
XLA Ops:
  0.6 0.8 %copy.16 = s32[8,2]{1,0:T(8,128)S(1)} copy(s32[8,2]{0,1:T(2,128)} %param.7) | data formatting | bytes 128 | tf_op args[1]
  1.4 0.1 eq.27
  1.5 0.1 stack_reshape.3
  1.6 0.2 convert_reduce_fusion
  1.8 0.1 copy.18
  1.9 0.1 reshape.34
  1.9 0.1 select_reduce_fusion
  2.0 0.7 %fusion.3 = bf16[2,128]{1,0:T(2,128)(2,1)S(1)} fusion(bf16[2,2]{1,0:T(2,128)(2,1)} %param.8, bf16[2,4]{1,0:T(2,128)(2,1)S(1)} %convert_element_type.9), kind=kLoop, calls=%fused_computation.10 | loop fusion | flops 1792 | bytes 536 | tf_op jit(solution)/shard_map/concatenate | solution.py:332
  2.8 0.7 %reshape.33 = bf16[16,512]{1,0:T(8,128)(2,1)S(1)} reshape(bf16[2,4096]{1,0:T(2,128)(2,1)} %param.6) | data formatting | bytes 32768 | tf_op jit(solution)/shard_map/reshape | solution.py:335
  3.5 0.6 %pad_maximum_fusion.payload = bf16[16,640]{1,0:T(8,128)(2,1)} fusion(bf16[16,128]{1,0:T(8,128)(2,1)S(1)} %broadcast_bitcast_fusion, bf16[16,512]{1,0:T(8,128)(2,1)S(1)} %reshape.33), kind=kLoop, calls=%fused_computation | loop fusion | flops 40960 | bytes 40960 | tf_op jit(solution)/shard_map/concatenate | solution.py:335
  4.1 33.9 %gather_project.1 = (bf16[2,32,4096]{2,1,0:T(8,128)(2,1)}, f32[2,32,128]{2,1,0:T(8,128)}, f32[2,24,1536]{2,1,0:T(8,128)}, f32[2,2]{1,0:T(2,128)}) custom-call(bf16[16,640]{1,0:T(8,128)(2,1)} %pad_maximum_fusion.payload, bf16[2,24,1536]{2,1,0:T(8,128)(2,1)} %gate_pre.3, bf16[2,24,1536]{2,1,0:T(8,128)(2,1)} %up_pre.3, bf16[2,1536,4096]{2,1,0:T(8,128)(2,1)} %weights.1), custom_call_target="tpu_custom_call" | custom-call | tf_op jit(solution)/shard_map/gather_project/pallas_call | solution.py:340
  38.0 14.7 %finish.1 = (bf16[2,24,1536]{2,1,0:T(8,128)(2,1)}, bf16[2,24,1536]{2,1,0:T(8,128)(2,1)}, bf16[2,1536,4096]{2,1,0:T(8,128)(2,1)}, f32[2,2]{1,0:T(2,128)}) custom-call(f32[2,24,1536]{2,1,0:T(8,128)} %get-tuple-element.12.proj, bf16[2,32,4096]{2,1,0:T(8,128)(2,1)} %get-tuple-element.13.rows_in, f32[2,32,128]{2,1,0:T(8,128)} %get-tuple-element.14.gates, ...), custom_call_target="tpu_custom_call" | custom-call | tf_op jit(solution)/shard_map/finish/pallas_call | solution.py:376
  (5 shorter events, 0.0 us)
